TPU v7x, 32 devices: a whole 2x2x4 slice. The times are simulated.
32 devices in a mesh: row: 4 (over y, x), col: 8 (over z, core).
Axes of the slice: x: 2, y: 2, z: 4, core: 2. Of those that a mesh axis runs over, the one named last changes fastest.
Arguments:
- amplitudes: bfloat16 [800, 800, 768], P('row', 'col'), may hold values from -6 to 6
- integrals: bfloat16 [800, 800, 256], P('row', 'col'), may hold values from -0.375 to 0.375
- window_index: int32 [256], replicated, may hold values from 0 to 639999, as said below
Outputs:
- residual: bfloat16 [800, 800, 768], P('row', 'col')
- pair_energy: float32 [768], replicated
Inputs may be any that keep to these rules, and one draw needn't show every extreme that they name: `window_index`: the window pairs are distinct; pair k lies in the block of a rows and b columns owned by device number k // 8 in row-major order of the (a, b) device grid, 8 pairs for each block.
All inputs are finite; a program needn't handle non-finite values.
Results may differ from a plain program's by a relative error of at most 0.001.
Values may be sent and summed in bfloat16 or wider, within the bound.
A program may use at most 256 MiB of HBM per device.

v0:
```python
import jax
import jax.numpy as jnp
from jax import lax
from jax.sharding import PartitionSpec as P


def shards(amplitudes, integrals, window_index):
    block_rows, block_cols, pairs = amplitudes.shape
    window = integrals.shape[2]
    ncols = lax.axis_size("col")
    nrows = lax.axis_size("row")
    per_device = window // (nrows * ncols)
    row_rank = lax.axis_index("row")
    col_rank = lax.axis_index("col")
    linear_rank = row_rank * ncols + col_rank
    owned_index = lax.dynamic_slice_in_dim(window_index, linear_rank * per_device, per_device)
    virtuals = block_rows * nrows
    row_offset = owned_index // virtuals - row_rank * block_rows
    col_offset = owned_index % virtuals - col_rank * block_cols
    owned = amplitudes[row_offset, col_offset]
    in_row = lax.all_gather(owned, "col", axis=0, tiled=True)
    columns = lax.all_gather(in_row, "row", axis=0, tiled=True)
    full = jnp.einsum("abk,kp->abp", integrals, columns, preferred_element_type=jnp.float32)
    partial_value = jnp.sum(amplitudes.astype(jnp.float32) * full, axis=(0, 1))
    pair_energy = lax.psum(partial_value, ("row", "col")) / virtuals
    residual = full.astype(jnp.bfloat16)
    return (residual, pair_energy)


def solution(mesh):
    return jax.shard_map(
        shards,
        mesh=mesh,
        in_specs=(P("row", "col", None), P("row", "col", None), P()),
        out_specs=(P("row", "col", None), P()),
        check_vma=False,
    )
```

profile of v0, /device:TPU:0, one launch (start us, length us, event | category | flops | bytes accessed | tf_op | source)
XLA Modules:
  0.0 172.8 jit_solution(1093921430304254708)
XLA Ops:
  0.6 0.8 fusion.7
  1.4 1.4 gather_fusion
  2.8 15.6 %all_gather.6 = bf16[64,768]{1,0:T(8,128)(2,1)S(1)} all-gather(bf16[8,768]{1,0:T(8,128)(2,1)S(1)} %gather_fusion), channel_id=1, replica_groups=mesh['row'=4,'col'=8] {'col'}, dimensions={0}, use_global_device_ids=true | all-gather | bytes 110592 | tf_op jit(solution)/shard_map/all_gather | solution.py:21
  18.4 9.5 %all_gather.7 = bf16[256,768]{1,0:T(8,128)(2,1)S(1)} all-gather(bf16[64,768]{1,0:T(8,128)(2,1)S(1)} %all_gather.6), channel_id=1, replica_groups=mesh['row'=4,'col'=8] {'row'}, dimensions={0}, use_global_device_ids=true | all-gather | bytes 491520 | tf_op jit(solution)/shard_map/all_gather | solution.py:22
  27.9 44.0 %bitcast_convert_fusion = (bf16[200,100,768]{2,1,0:T(8,128)(2,1)}, f32[768,200,100]{0,2,1:T(8,128)}) fusion(bf16[200,100,256]{2,0,1:T(8,128)(2,1)} %param.4, bf16[256,768]{1,0:T(8,128)(2,1)S(1)} %all_gather.7), kind=kOutput, calls=%fused_computation.2 | convolution fusion | flops 7879680000 | bytes 102793216 | tf_op jit(solution)/shard_map/abk,kp->abp/dot_general | solution.py:23
  71.9 22.0 %copy.7 = bf16[200,100,768]{2,0,1:T(8,128)(2,1)} copy(bf16[200,100,768]{2,1,0:T(8,128)(2,1)} %get-tuple-element.4) | data formatting | bytes 61440000
  93.9 39.0 %fusion = f32[768]{0:T(1024)S(1)} fusion(f32[768,200,100]{0,2,1:T(8,128)} %get-tuple-element.5, bf16[200,100,768]{2,0,1:T(8,128)(2,1)} %param.3), kind=kLoop, calls=%fused_computation.3 | loop fusion | flops 46079232 | bytes 92163072 | tf_op jit(solution)/shard_map/reduce_sum | solution.py:24
  132.9 39.3 %psum.7 = f32[768]{0:T(1024)S(1)} all-reduce(f32[768]{0:T(1024)S(1)} %fusion), channel_id=1, replica_groups=mesh['row'=4,'col'=8] {'row','col'}, use_global_device_ids=true, to_apply=%region_1.2 | all-reduce | flops 768 | bytes 6144 | tf_op jit(solution)/shard_map/psum | solution.py:25
  172.2 0.6 broadcast_multiply_fusion
where the time goes:
time: 173 us
  blocking collectives  64.5 us (37%)
  matrix products  44 us (25%)
  other arithmetic  40.3 us (23%)
  local copies, waits for them, and re-layouts  23.3 us (13%)
    dot_general x1, matrix products, shards(): jnp.einsum('abk,kp->abp', integrals, columns, preferred_element_type=jnp....  44 us
    psum x1, blocking collectives, shards(): pair_energy = lax.psum(partial_value, ('row', 'col')) / virtuals  39.3 us
    reduce_sum x1, other arithmetic, shards(): partial_value = jnp.sum(amplitudes.astype(jnp.float32) * full, axis=(0, 1))  39 us
    unnamed x1, local copies, waits for them, and re-layouts  22 us
    all_gather x1, blocking collectives, shards(): in_row = lax.all_gather(owned, 'col', axis=0, tiled=True)  15.6 us
    all_gather x1, blocking collectives, shards(): columns = lax.all_gather(in_row, 'row', axis=0, tiled=True)  9.5 us

commit v1 on v0

--- a/solution.py
+++ b/solution.py
@@ -22,7 +22,7 @@
     columns = lax.all_gather(in_row, "row", axis=0, tiled=True)
     full = jnp.einsum("abk,kp->abp", integrals, columns, preferred_element_type=jnp.float32)
     partial_value = jnp.sum(amplitudes.astype(jnp.float32) * full, axis=(0, 1))
-    pair_energy = lax.psum(partial_value, ("row", "col")) / virtuals
+    pair_energy = lax.psum(lax.psum(partial_value, "col"), "row") / virtuals
     residual = full.astype(jnp.bfloat16)
     return (residual, pair_energy)
 

time: 173 us -> 158 us (0.913)
  blocking collectives: 64.5 us -> 49 us
    psum x1 -> x2, blocking collectives: 39.3 us -> 23.9 us  [shards(): pair_energy = lax.psum(lax.psum(partial_value, 'col'), 'row') / virtuals]
where the time goes in v1:
time: 158 us; the launch traced here: 157 us
  blocking collectives  49 us (31%)
  matrix products  44 us (28%)
  other arithmetic  40.3 us (26%)
  local copies, waits for them, and re-layouts  23.3 us (15%)
    dot_general x1, matrix products, shards(): jnp.einsum('abk,kp->abp', integrals, columns, preferred_element_type=jnp....  44 us
    reduce_sum x1, other arithmetic, shards(): partial_value = jnp.sum(amplitudes.astype(jnp.float32) * full, axis=(0, 1))  39 us
    psum x2, blocking collectives, shards(): pair_energy = lax.psum(lax.psum(partial_value, 'col'), 'row') / virtuals  23.9 us
    unnamed x1, local copies, waits for them, and re-layouts  22 us
    all_gather x1, blocking collectives, shards(): in_row = lax.all_gather(owned, 'col', axis=0, tiled=True)  15.6 us
    all_gather x1, blocking collectives, shards(): columns = lax.all_gather(in_row, 'row', axis=0, tiled=True)  9.5 us

profile of v1, /device:TPU:0, one launch (start us, length us, event | category | flops | bytes accessed | tf_op | source)
XLA Modules:
  0.0 157.3 jit_solution(8882188267111788631)
XLA Ops:
  0.6 0.8 fusion.7
  1.4 1.4 gather_fusion
  2.8 15.6 %all_gather.6 = bf16[64,768]{1,0:T(8,128)(2,1)S(1)} all-gather(bf16[8,768]{1,0:T(8,128)(2,1)S(1)} %gather_fusion), channel_id=1, replica_groups=mesh['row'=4,'col'=8] {'col'}, dimensions={0}, use_global_device_ids=true | all-gather | bytes 110592 | tf_op jit(solution)/shard_map/all_gather | solution.py:21
  18.4 9.5 %all_gather.7 = bf16[256,768]{1,0:T(8,128)(2,1)S(1)} all-gather(bf16[64,768]{1,0:T(8,128)(2,1)S(1)} %all_gather.6), channel_id=1, replica_groups=mesh['row'=4,'col'=8] {'row'}, dimensions={0}, use_global_device_ids=true | all-gather | bytes 491520 | tf_op jit(solution)/shard_map/all_gather | solution.py:22
  27.9 44.0 %bitcast_convert_fusion = (bf16[200,100,768]{2,1,0:T(8,128)(2,1)}, f32[768,200,100]{0,2,1:T(8,128)}) fusion(bf16[200,100,256]{2,0,1:T(8,128)(2,1)} %param.4, bf16[256,768]{1,0:T(8,128)(2,1)S(1)} %all_gather.7), kind=kOutput, calls=%fused_computation.2 | convolution fusion | flops 7879680000 | bytes 102793216 | tf_op jit(solution)/shard_map/abk,kp->abp/dot_general | solution.py:23
  71.9 22.0 %copy.7 = bf16[200,100,768]{2,0,1:T(8,128)(2,1)} copy(bf16[200,100,768]{2,1,0:T(8,128)(2,1)} %get-tuple-element.4) | data formatting | bytes 61440000
  93.9 39.0 %fusion = f32[768]{0:T(1024)S(1)} fusion(f32[768,200,100]{0,2,1:T(8,128)} %get-tuple-element.5, bf16[200,100,768]{2,0,1:T(8,128)(2,1)} %param.3), kind=kLoop, calls=%fused_computation.3 | loop fusion | flops 46079232 | bytes 92163072 | tf_op jit(solution)/shard_map/reduce_sum | solution.py:24
  132.9 14.9 %psum.14 = f32[768]{0:T(1024)S(1)} all-reduce(f32[768]{0:T(1024)S(1)} %fusion), channel_id=1, replica_groups=mesh['row'=4,'col'=8] {'col'}, use_global_device_ids=true, to_apply=%region_1.2 | all-reduce | flops 768 | bytes 6144 | tf_op jit(solution)/shard_map/psum | solution.py:25
  147.8 9.0 %psum.15 = f32[768]{0:T(1024)S(1)} all-reduce(f32[768]{0:T(1024)S(1)} %psum.14), channel_id=1, replica_groups=mesh['row'=4,'col'=8] {'row'}, use_global_device_ids=true, to_apply=%region_2.3 | all-reduce | flops 768 | bytes 6144 | tf_op jit(solution)/shard_map/psum | solution.py:25
  156.7 0.6 broadcast_multiply_fusion

commit v2 on v0

--- a/solution.py
+++ b/solution.py
@@ -19,7 +19,9 @@
     col_offset = owned_index % virtuals - col_rank * block_cols
     owned = amplitudes[row_offset, col_offset]
     in_row = lax.all_gather(owned, "col", axis=0, tiled=True)
-    columns = lax.all_gather(in_row, "row", axis=0, tiled=True)
+    columns = jnp.concatenate(
+        lax.all_to_all(jnp.stack([in_row] * lax.axis_size("row")), "row", 0, 0), axis=0
+    )
     full = jnp.einsum("abk,kp->abp", integrals, columns, preferred_element_type=jnp.float32)
     partial_value = jnp.sum(amplitudes.astype(jnp.float32) * full, axis=(0, 1))
     pair_energy = lax.psum(partial_value, ("row", "col")) / virtuals

time: 173 us -> 175 us (1.012)
    all_to_all x0 -> x1, blocking collectives: none -> 11.1 us  [shards(): lax.all_to_all(jnp.stack([in_row] * lax.axis_size('row')), 'row', 0, 0)]
    all_gather x1 -> x0, blocking collectives: 9.5 us -> none  [shards(): columns = lax.all_gather(in_row, 'row', axis=0, tiled=True)]
where the time goes in v2:
time: 175 us; the launch traced here: 174 us
  blocking collectives  66.1 us (38%)
  matrix products  44 us (25%)
  other arithmetic  40.3 us (23%)
  local copies, waits for them, and re-layouts  23.4 us (13%)
    dot_general x1, matrix products, shards(): jnp.einsum('abk,kp->abp', integrals, columns, preferred_element_type=jnp....  44 us
    psum x1, blocking collectives, shards(): pair_energy = lax.psum(partial_value, ('row', 'col')) / virtuals  39.3 us
    reduce_sum x1, other arithmetic, shards(): partial_value = jnp.sum(amplitudes.astype(jnp.float32) * full, axis=(0, 1))  39 us
    unnamed x1, local copies, waits for them, and re-layouts  22 us
    all_gather x1, blocking collectives, shards(): in_row = lax.all_gather(owned, 'col', axis=0, tiled=True)  15.6 us
    all_to_all x1, blocking collectives, shards(): lax.all_to_all(jnp.stack([in_row] * lax.axis_size('row')), 'row', 0, 0)  11.1 us

profile of v2, /device:TPU:0, one launch (start us, length us, event | category | flops | bytes accessed | tf_op | source)
XLA Modules:
  0.0 174.4 jit_solution(2745551312663706725)
XLA Ops:
  0.6 0.8 fusion.6
  1.4 1.4 gather_fusion
  2.8 15.6 %all_gather.3 = bf16[64,768]{1,0:T(8,128)(2,1)S(1)} all-gather(bf16[8,768]{1,0:T(8,128)(2,1)S(1)} %gather_fusion), channel_id=1, replica_groups=mesh['row'=4,'col'=8] {'col'}, dimensions={0}, use_global_device_ids=true | all-gather | bytes 110592 | tf_op jit(solution)/shard_map/all_gather | solution.py:21
  18.4 11.1 %all_to_all.5 = bf16[4,64,768]{2,1,0:T(8,128)(2,1)S(1)} all-to-all(bf16[4,64,768]{2,1,0:T(8,128)(2,1)S(1)} %stack.2), channel_id=1, replica_groups=mesh['row'=4,'col'=8] {'row'}, dimensions={0} | all-to-all | bytes 786432 | tf_op jit(solution)/shard_map/all_to_all | solution.py:23
  29.6 44.0 %bitcast_convert_fusion = (bf16[200,100,768]{2,1,0:T(8,128)(2,1)}, f32[768,200,100]{0,2,1:T(8,128)}) fusion(bf16[256,768,1]{1,0,2:T(8,128)(2,1)S(1)} %bitcast.9, bf16[200,100,256]{2,0,1:T(8,128)(2,1)} %param.4), kind=kOutput, calls=%fused_computation.2 | convolution fusion | flops 7879680000 | bytes 102793216 | tf_op jit(solution)/shard_map/abk,kp->abp/dot_general | solution.py:25
  73.6 22.0 %copy.7 = bf16[200,100,768]{2,0,1:T(8,128)(2,1)} copy(bf16[200,100,768]{2,1,0:T(8,128)(2,1)} %get-tuple-element.4) | data formatting | bytes 61440000
  95.6 39.0 %fusion = f32[768]{0:T(1024)S(1)} fusion(f32[768,200,100]{0,2,1:T(8,128)} %get-tuple-element.5, bf16[200,100,768]{2,0,1:T(8,128)(2,1)} %param.3), kind=kLoop, calls=%fused_computation.3 | loop fusion | flops 46079232 | bytes 92163072 | tf_op jit(solution)/shard_map/reduce_sum | solution.py:26
  134.5 39.3 %psum.7 = f32[768]{0:T(1024)S(1)} all-reduce(f32[768]{0:T(1024)S(1)} %fusion), channel_id=1, replica_groups=mesh['row'=4,'col'=8] {'row','col'}, use_global_device_ids=true, to_apply=%region_1.2 | all-reduce | flops 768 | bytes 6144 | tf_op jit(solution)/shard_map/psum | solution.py:27
  173.8 0.6 broadcast_multiply_fusion
  (1 shorter events, 0.0 us)
